TPU v7x, 32 devices: a whole 2x2x4 slice. The times are simulated.
32 devices in a mesh: replica: 4 (over z), fsdp: 8 (over y, x, core).
Axes of the slice: x: 2, y: 2, z: 4, core: 2. Of those that a mesh axis runs over, the one named last changes fastest.
Arguments:
- states: bfloat16 [32, 256, 2048], P(('replica', 'fsdp'))
- cotangent: bfloat16 [32, 256, 512], P(('replica', 'fsdp')), may hold values from -6 to 6
- kv_weight: bfloat16 [2048, 512], P('fsdp'), may hold values from -0.125 to 0.125
- norm_gain: bfloat16 [2048], P('fsdp'), may hold values from -1.5 to 1.5
- prompt_len: int32 [32], P(('replica', 'fsdp')), may hold values from 1 to 255, as said below
- response_len: int32 [32], P(('replica', 'fsdp')), may hold values from 1 to 192
- reward_bucket: int32 [32], P(('replica', 'fsdp')), may hold values from 0 to 10, as said below
Outputs:
- key_values: bfloat16 [32, 256, 512], P(('replica', 'fsdp'))
- grad_weight: float32 [2048, 512], P('fsdp')
- grad_gain: float32 [2048], P('fsdp')
Inputs may be any that keep to these rules, and one draw needn't show every extreme that they name: prompt_len + response_len <= 256 for every rollout. `reward_bucket`: some rollout has level 0 and some has level 10.
All inputs are finite; a program needn't handle non-finite values.
Results may differ from a plain program's by a relative error of at most 0.005.
Values may be sent and summed in bfloat16 or wider, within the bound.
A program may use at most 64 MiB of HBM per device.

v0:
```python
import functools

import jax
import jax.numpy as jnp
from jax import lax
from jax.experimental import pallas as pl
from jax.experimental.pallas import tpu as pltpu
from jax.sharding import PartitionSpec as P

EPSILON = 1e-06
MESH = pl.DeviceIdType.MESH
BF = jnp.bfloat16
F32 = jnp.float32
TILE = 256


def flip(me, mask):
    out = me
    bit = 0
    while mask >> bit:
        if (mask >> bit) & 1:
            own = lax.rem(lax.div(me, 1 << bit), 2)
            out = out + (1 - 2 * own) * (1 << bit)
        bit += 1
    return out


def offset_of(position, order):
    count = len(order)
    return sum(((position >> (count - 1 - i)) & 1) << order[i] for i in range(count))


def kernel(
    R, F, chunk_rows,
    states_hbm, cot_hbm, weight_hbm, gain_ref, prompt_ref, response_ref, reward_ref,
    kv_ref, gw_ref, gg_ref,
    states, cot, normed, live_cot, inverse, w_rel, w_nat, grad, sending, receiving,
    gain_rel, gain_nat, scal_out, scal_in, zscal, gvec, gg_out, gg_in, gg_row, zgg,
    own, chain_out, chain_in,
    load_sem, send_sem, recv_sem,
):
    r, f = lax.axis_index("replica"), lax.axis_index("fsdp")
    bits = F.bit_length() - 1
    rest = list(range(1, bits))
    orders = ([0] + rest if bits else [], [0] + rest[::-1] if bits else [])
    rows, half = w_rel.shape[2], w_rel.shape[3]
    seq, width = states.shape
    row_parts = rows // chunk_rows
    chunks = 2 * row_parts
    tiles = width // TILE
    counter = [2 * chunks]
    pending = []

    def remote(src, dst, device):
        index = counter[0]
        counter[0] += 1
        copy = pltpu.make_async_remote_copy(
            src_ref=src, dst_ref=dst, send_sem=send_sem.at[index], recv_sem=recv_sem.at[index],
            device_id=device, device_id_type=MESH,
        )
        copy.start()
        pending.append(copy)
        return copy

    def across(bit):
        return (r, flip(f, 1 << bit))

    w_loads = []
    for p in range(2):
        w_loads.append(
            pltpu.make_async_copy(
                weight_hbm.at[:, pl.ds(p * half, half)], w_rel.at[p, 0], load_sem.at[p]
            )
        )
    state_load = pltpu.make_async_copy(states_hbm.at[0], states, load_sem.at[2])
    cot_load = pltpu.make_async_copy(cot_hbm.at[0], cot, load_sem.at[3])
    for copy in w_loads + [state_load, cot_load]:
        copy.start()

    gain_rel[0] = gain_ref[...].astype(F32)
    lane = lax.broadcasted_iota(jnp.int32, (8, 128), 1)
    reward = reward_ref[0].astype(F32)
    tokens = response_ref[0].astype(F32)
    zero = jnp.zeros((8, 128), F32)
    scal = jnp.where(lane == 0, zero + reward, zero)
    scal = jnp.where(lane == 1, zero + reward * reward, scal)
    scal = jnp.where(lane == 2, zero + tokens, scal)

    @pl.when(r == 0)
    def _():
        chain_in[0] = jnp.zeros(chain_in.shape[1:], chain_in.dtype)

    @pl.when(r == R - 1)
    def _():
        chain_in[1] = jnp.zeros(chain_in.shape[1:], chain_in.dtype)

    barrier = pltpu.get_barrier_semaphore()
    for bit in range(bits):
        pl.semaphore_signal(barrier, inc=1, device_id=across(bit), device_id_type=MESH)
    for k in range(1, R):
        pl.semaphore_signal(barrier, inc=1, device_id=(lax.rem(r + k, R), f), device_id_type=MESH)
    pl.semaphore_wait(barrier, bits + R - 1)

    def small_send(step, scal):
        bit = orders[0][bits - 1 - step]
        held = 1 << step
        scal_out[step] = scal
        return (
            remote(gain_rel.at[pl.ds(0, held)], gain_rel.at[pl.ds(held, held)], across(bit)),
            remote(scal_out.at[step], scal_in.at[step], across(bit)),
        )

    def small_wait(step, scal, copies):
        for copy in copies:
            copy.wait_recv()
        return scal + scal_in[step]

    def weight_send(step):
        held = 1 << step
        return [
            remote(
                w_rel.at[p, pl.ds(0, held)], w_rel.at[p, pl.ds(held, held)],
                across(orders[p][bits - 1 - step]),
            )
            for p in range(2)
        ]

    small = small_send(0, scal) if bits else None
    for copy in w_loads:
        copy.wait()
    moving = weight_send(0) if bits else []
    state_load.wait()

    def square_tile(i, total):
        part = states[:, pl.ds(pl.multiple_of(i * TILE, TILE), TILE)].astype(F32)
        return total + jnp.sum(part * part, axis=1, keepdims=True)

    squares = lax.fori_loop(0, tiles, square_tile, jnp.zeros((seq, 1), F32))
    inverse[...] = lax.rsqrt(squares / width + EPSILON)
    cot_load.wait()
    position = lax.broadcasted_iota(jnp.int32, (seq, cot.shape[1]), 0)
    first = prompt_ref[0]
    alive = (position >= first) & (position < first + response_ref[0])
    live_cot[...] = jnp.where(alive, cot[...].astype(F32), 0.0).astype(BF)

    for step in range(bits):
        scal = small_wait(step, scal, small)
        if step + 1 < bits:
            small = small_send(step + 1, scal)
        if step == 0 and bits > 1:
            for copy in moving:
                copy.wait_recv()
            moving = weight_send(1)

    scal_out[bits] = scal
    zcopies = [
        remote(scal_out.at[bits], zscal.at[k - 1], (lax.rem(r + k, R), f)) for k in range(1, R)
    ]
    for q in range(F):
        gain_nat[flip(f, offset_of(q, orders[0]))] = gain_rel[q]
    for b in range(F):
        gvec[:, b * rows:(b + 1) * rows] = gain_nat[b]

    def grad_tile(i, carry):
        at = pl.ds(pl.multiple_of(i * TILE, TILE), TILE)
        unit = states[:, at].astype(F32) * inverse[...]
        part = (unit * (1.0 + gvec[:, at])).astype(BF)
        normed[:, at] = part
        grad[at, :] = lax.dot_general(
            part, live_cot[...], (((0,), (0,)), ((), ())), preferred_element_type=F32
        )
        return carry

    lax.fori_loop(0, tiles, grad_tile, 0)

    for copy in zcopies:
        copy.wait_recv()
    for k in range(R - 1):
        scal = scal + zscal[k]
    count = float(R * F)

    def pick(which):
        return jnp.sum(jnp.where(lane[0:1] == which, scal[0:1], 0.0), axis=1, keepdims=True)

    average = pick(0) / count
    variance = pick(1) / count - average * average
    coef = (reward - average) * (lax.rsqrt(variance + EPSILON) * lax.rsqrt(pick(2)))

    starts = [F - (F >> i) for i in range(bits + 1)]

    def partial(p, q, step):
        begin = pl.multiple_of(flip(f, offset_of(q, orders[p])) * rows, rows)
        value = grad[pl.ds(begin, rows), p * half:(p + 1) * half] * coef
        for i in range(step):
            value = value + receiving[p, starts[i] + q].astype(F32)
        return value

    def scatter_send(p, step):
        keep = F >> (step + 1)
        for q in range(keep):
            sending[p, starts[step] + q] = partial(p, keep + q, step).astype(BF)
        at = pl.ds(starts[step], keep)
        return remote(sending.at[p, at], receiving.at[p, at], across(orders[p][step]))

    shares = [scatter_send(p, 0) for p in range(2)] if bits else []
    if bits > 1:
        for p in range(2):
            shares[p].wait_recv()
            shares[p] = scatter_send(p, 1)
    for step in range(2, bits):
        for copy in moving:
            copy.wait_recv()
        moving = weight_send(step)
    for p in range(2):
        if bits:
            moving[p].wait_recv()
        for q in range(F):
            begin = pl.multiple_of(flip(f, offset_of(q, orders[p])) * rows, rows)
            w_nat[pl.ds(begin, rows), p * half:(p + 1) * half] = w_rel[p, q]

    def gain_tile(i, carry):
        at = pl.ds(pl.multiple_of(i * TILE, TILE), TILE)
        backward = lax.dot_general(
            live_cot[...], w_nat[at, :], (((1,), (1,)), ((), ())), preferred_element_type=F32
        )
        unit = states[:, at].astype(F32) * inverse[...]
        gvec[:, at] = jnp.sum(unit * backward, axis=0, keepdims=True) * coef
        return carry

    lax.fori_loop(0, tiles, gain_tile, 0)
    for b in range(F):
        gg_out[0, b] = gvec[:, b * rows:(b + 1) * rows]
    gains = remote(gg_out.at[0], gg_in.at[0], across(0)) if bits else None
    kv_ref[0] = jnp.dot(normed[...], w_nat[...], preferred_element_type=F32).astype(BF)

    def gains_next(step):
        gains.wait_recv()
        gg_out[step] = gg_out[step - 1] + gg_in[step - 1]
        if step < bits:
            return remote(gg_out.at[step], gg_in.at[step], across(step))
        return None

    for step in range(2, bits):
        for p in range(2):
            shares[p].wait_recv()
            shares[p] = scatter_send(p, step)
        gains = gains_next(step - 1)

    near = lax.div(2 * r, R)

    def relay(way, c):
        step = 1 - 2 * way
        before, after = r - step, r + step
        has_before = (before >= 0) & (before < R)
        has_after = (after >= 0) & (after < R)
        index = way * chunks + c
        copy = pltpu.make_async_remote_copy(
            src_ref=chain_out.at[way, c], dst_ref=chain_in.at[way, c],
            send_sem=send_sem.at[index], recv_sem=recv_sem.at[index],
            device_id=(lax.rem(after + R, R), f), device_id_type=MESH,
        )

        @pl.when(has_before)
        def _():
            copy.wait_recv()

        @pl.when(has_after)
        def _():
            chain_out[way, c] = (own[c] + chain_in[way, c].astype(F32)).astype(chain_out.dtype)
            copy.start()

        return has_after, copy

    sent = []
    for p in range(2):
        if bits:
            shares[p].wait_recv()
        value = partial(p, 0, bits)
        for k in range(row_parts):
            own[p * row_parts + k] = value[k * chunk_rows:(k + 1) * chunk_rows]
    lead = chunks
    for c in range(lead):
        sent.append(relay(near, c))
    if bits > 1:
        gains = gains_next(bits - 1)
    for c in range(chunks):
        sent.append(relay(1 - near, c))
        if c == 0:
            if bits:
                gains_next(bits)
            gg_row[...] = gg_out[bits, f]
            zgains = [
                remote(gg_row, zgg.at[k - 1], (lax.rem(r + k, R), f)) for k in range(1, R)
            ]
        if c + lead < chunks:
            sent.append(relay(near, c + lead))
        p, k = c // row_parts, c % row_parts
        gw_ref[k * chunk_rows:(k + 1) * chunk_rows, p * half:(p + 1) * half] = (
            own[c] + chain_in[0, c].astype(F32) + chain_in[1, c].astype(F32)
        )
    total = gg_row[...]
    for k in range(R - 1):
        zgains[k].wait_recv()
        total = total + zgg[k]
    gg_ref[...] = total
    for copy in pending:
        copy.wait_send()
    for has_after, copy in sent:
        @pl.when(has_after)
        def _(copy=copy):
            copy.wait_send()


def shards(R, F, states, cotangent, kv_weight, norm_gain, prompt_len, response_len, reward_bucket):
    _, seq, width = states.shape
    rows, features = kv_weight.shape
    half = features // 2
    bits = F.bit_length() - 1
    chunk_rows = max(rows // 2, min(rows, 32))
    chunks = 2 * (rows // chunk_rows)
    wire = BF if R <= 4 else F32
    semaphores = 2 * chunks + 7 * bits + 2 * (R - 1)
    zs = max(R - 1, 1)
    bs = max(bits, 1)
    vmem = pl.BlockSpec(memory_space=pltpu.VMEM)
    smem = pl.BlockSpec(memory_space=pltpu.SMEM)
    hbm = pl.BlockSpec(memory_space=pl.ANY)
    key_values, grad_weight, grad_gain = pl.pallas_call(
        functools.partial(kernel, R, F, chunk_rows),
        out_shape=(
            jax.ShapeDtypeStruct((1, seq, features), BF),
            jax.ShapeDtypeStruct((rows, features), F32),
            jax.ShapeDtypeStruct((1, rows), F32),
        ),
        in_specs=[hbm, hbm, hbm, vmem, smem, smem, smem],
        out_specs=(vmem, vmem, vmem),
        scratch_shapes=[
            pltpu.VMEM((seq, width), BF),
            pltpu.VMEM((seq, features), BF),
            pltpu.VMEM((seq, width), BF),
            pltpu.VMEM((seq, features), BF),
            pltpu.VMEM((seq, 1), F32),
            pltpu.VMEM((2, F, rows, half), BF),
            pltpu.VMEM((width, features), BF),
            pltpu.VMEM((width, features), F32),
            pltpu.VMEM((2, F, rows, half), BF),
            pltpu.VMEM((2, F, rows, half), BF),
            pltpu.VMEM((F, 1, rows), F32),
            pltpu.VMEM((F, 1, rows), F32),
            pltpu.VMEM((bits + 1, 8, 128), F32),
            pltpu.VMEM((bs, 8, 128), F32),
            pltpu.VMEM((zs, 8, 128), F32),
            pltpu.VMEM((1, width), F32),
            pltpu.VMEM((bits + 1, F, 1, rows), F32),
            pltpu.VMEM((bs, F, 1, rows), F32),
            pltpu.VMEM((1, rows), F32),
            pltpu.VMEM((zs, 1, rows), F32),
            pltpu.VMEM((chunks, chunk_rows, half), F32),
            pltpu.VMEM((2, chunks, chunk_rows, half), wire),
            pltpu.VMEM((2, chunks, chunk_rows, half), wire),
            pltpu.SemaphoreType.DMA((4,)),
            pltpu.SemaphoreType.DMA((semaphores,)),
            pltpu.SemaphoreType.DMA((semaphores,)),
        ],
        compiler_params=pltpu.CompilerParams(
            collective_id=0, has_side_effects=True, vmem_limit_bytes=56 * 1024 * 1024
        ),
    )(states, cotangent, kv_weight, norm_gain.reshape(1, rows), prompt_len, response_len, reward_bucket)
    return key_values, grad_weight, grad_gain.reshape(rows)


def solution(mesh):
    placed = (
        P(("replica", "fsdp"), None, None),
        P(("replica", "fsdp"), None, None),
        P("fsdp", None),
        P("fsdp"),
        P(("replica", "fsdp")),
        P(("replica", "fsdp")),
        P(("replica", "fsdp")),
    )
    return jax.shard_map(
        functools.partial(shards, mesh.shape["replica"], mesh.shape["fsdp"]),
        mesh=mesh,
        in_specs=placed,
        out_specs=(P(("replica", "fsdp"), None, None), P("fsdp", None), P("fsdp")),
        check_vma=False,
    )
```

profile of v0, /device:TPU:0, one launch (start us, length us, event | category | flops | bytes accessed | tf_op | source)
XLA Modules:
  0.0 51.7 jit_solution(170428310721617491)
XLA Ops:
  1.9 0.0 copy-start.2
  2.6 0.0 copy-done.2
  2.6 0.6 %reshape.12.gain_ref = bf16[1,256]{1,0:T(2,128)(2,1)} reshape(bf16[256]{0:T(256)(128)(2,1)S(1)} %copy-done.2) | data formatting | bytes 1024 | tf_op jit(solution)/shard_map/reshape | solution.py:368
  3.2 45.4 %shard_map.94 = (bf16[1,256,512]{2,1,0:T(8,128)(2,1)}, f32[256,512]{1,0:T(8,128)}, f32[1,256]{1,0:T(1,128)}) custom-call(bf16[1,256,2048]{2,1,0:T(8,128)(2,1)} %states_hbm.1, bf16[1,256,512]{2,1,0:T(8,128)(2,1)} %cot_hbm.1, bf16[256,512]{1,0:T(8,128)(2,1)} %weight_hbm.1, bf16[1,256]{1,0:T(2,128)(2,1)} %reshape.12.gain_ref, s32[1]{0:T(128)S(6)} %copy.13.prompt_ref, ...), custom_call_target="tpu_custom_call" | custom-call | tf_op jit(solution)/shard_map/pallas_call | solution.py:328
  48.6 0.0 copy-start
  48.6 1.7 %copy.16 = bf16[1,256,512]{2,1,0:T(8,128)(2,1)} copy(bf16[1,256,512]{2,1,0:T(8,128)(2,1)} %get-tuple-element.12) | data formatting | bytes 524288
  50.3 0.0 copy-done
  50.3 0.0 copy-start.1
  50.3 0.8 %copy.17 = f32[256,512]{1,0:T(8,128)} copy(f32[256,512]{1,0:T(8,128)S(1)} %copy-done) | data formatting | bytes 1048576
  51.1 0.0 copy-done.1
  51.1 0.6 %copy.18 = f32[256]{0:T(256)} copy(f32[256]{0:T(256)S(1)} %bitcast.1) | data formatting | bytes 2048
Async XLA Ops:
  1.9 0.7 %copy-start.2 = (bf16[256]{0:T(256)(128)(2,1)S(1)}, bf16[256]{0:T(256)(128)(2,1)}, u32[]{:S(2)}) copy-start(bf16[256]{0:T(256)(128)(2,1)} %param.10) | copy-start | bytes 1540
  48.6 1.7 %copy-start = (f32[256,512]{1,0:T(8,128)S(1)}, f32[256,512]{1,0:T(8,128)}, u32[]{:S(2)}) copy-start(f32[256,512]{1,0:T(8,128)} %get-tuple-element.13) | copy-start | bytes 1572868
  50.3 0.8 %copy-start.1 = (f32[1,256]{1,0:T(1,128)S(1)}, f32[1,256]{1,0:T(1,128)}, u32[]{:S(2)}) copy-start(f32[1,256]{1,0:T(1,128)} %get-tuple-element.8) | copy-start | bytes 3076
where the time goes:
time: 51.9 us; the launch traced here: 51.7 us
  Pallas kernels  45.4 us (87%)
  local copies, waits for them, and re-layouts  3.66 us (7%)
  between operations  2.62 us (5%)
    pallas_call x1, Pallas kernels, shards(): pl.pallas_call(functools.partial(kernel, R, F, chunk_rows), out_shape=(ja...  45.4 us
    unnamed x9, local copies, waits for them, and re-layouts  3.1 us

commit v1 on v0

v1 whole, which is shorter than its diff:
```python
import functools

import jax
import jax.numpy as jnp
from jax import lax
from jax.experimental import pallas as pl
from jax.experimental.pallas import tpu as pltpu
from jax.sharding import PartitionSpec as P

EPSILON = 1e-06
MESH = pl.DeviceIdType.MESH
BF = jnp.bfloat16
F32 = jnp.float32
TILE = 256
HOP = 8


def flip(me, mask):
    out = me
    bit = 0
    while mask >> bit:
        if (mask >> bit) & 1:
            own = lax.rem(lax.div(me, 1 << bit), 2)
            out = out + (1 - 2 * own) * (1 << bit)
        bit += 1
    return out


def offset_of(position, order):
    count = len(order)
    return sum(((position >> (count - 1 - i)) & 1) << order[i] for i in range(count))


def plan(R, F):
    bits = F.bit_length() - 2
    count = 1 << bits
    everyone = [(k, m) for k in range(R) for m in range(count) if k or m]
    if R * count <= 32:
        stages = [everyone]
    else:
        stages = [[e for e in everyone if not e[0]], [e for e in everyone if not e[1]]]
    return bits, count, stages


def kernel(
    R, F, chunk_rows,
    states_hbm, cot_hbm, weight_hbm, gain_hbm, prompt_ref, response_ref, reward_ref,
    kv_ref, gw_ref, gg_ref,
    states, cot, scaled, weight, w_all, gain,
    grad, grad_send, grad_in, sending, receiving, own, chain_out, chain_in,
    fin_out, fin_in, scal_out, scal_pair, scal_in, acc, inverse, gcol, wide_gain,
    load_sem, w_send, w_recv, fw_send, fw_recv, g_send, g_recv, x_send, x_recv,
    z_send, z_recv, fin_send, fin_recv, s_send, s_recv, gate,
):
    r, f = lax.axis_index("replica"), lax.axis_index("fsdp")
    bits, count, stages = plan(R, F)
    orders = (list(range(bits)), list(range(bits))[::-1])
    j = lax.div(f, 2)
    odd = lax.rem(f, 2) == 1
    seq, width = states.shape
    features = cot.shape[1]
    half = features // 2
    rows = weight.shape[0]
    pair = 2 * rows
    tiles = width // TILE
    chunks = pair // chunk_rows
    partner = (r, flip(f, 1))
    pending = []

    def remote(src, dst, send_sem, recv_sem, device):
        return pltpu.make_async_remote_copy(
            src_ref=src, dst_ref=dst, send_sem=send_sem, recv_sem=recv_sem,
            device_id=device, device_id_type=MESH,
        )

    def launch(copy):
        copy.start()
        pending.append(copy)
        return copy

    def finish():
        for copy in pending:
            copy.wait_send()
        pending.clear()

    def across(bit):
        return (r, flip(f, 2 << bit))

    def peer(k, m):
        return (lax.rem(r + k, R), flip(f, m << 1))

    def pair_begin(m):
        return pl.multiple_of(flip(j, m) * pair, pair)

    loads = [
        pltpu.make_async_copy(src, dst, load_sem.at[i])
        for i, (src, dst) in enumerate([
            (gain_hbm, gain), (weight_hbm, weight), (states_hbm.at[0], states), (cot_hbm.at[0], cot),
        ])
    ]
    for copy in loads:
        copy.start()
    gain_load, weight_load, states_load, cot_load = loads

    barrier = pltpu.get_barrier_semaphore()
    pl.semaphore_signal(barrier, inc=1, device_id=partner, device_id_type=MESH)
    peers = [e for stage in stages for e in stage]

    @pl.when(odd)
    def _():
        for k, m in peers:
            pl.semaphore_signal(barrier, inc=1, device_id=peer(k, m), device_id_type=MESH)

    @pl.when(jnp.logical_not(odd))
    def _():
        for bit in range(bits):
            pl.semaphore_signal(barrier, inc=1, device_id=across(bit), device_id_type=MESH)

    lane = lax.broadcasted_iota(jnp.int32, (1, 128), 1)
    diagonal = lax.broadcasted_iota(jnp.int32, (rows, rows), 0) == lax.broadcasted_iota(
        jnp.int32, (rows, rows), 1
    )
    mine = pl.multiple_of(f * rows, rows)

    def scalars():
        reward = reward_ref[0].astype(F32)
        tokens = response_ref[0].astype(F32)
        zero = jnp.zeros((1, 128), F32)
        out = jnp.where(lane == 0, zero + reward, zero)
        out = jnp.where(lane == 1, zero + reward * reward, out)
        return jnp.where(lane == 2, zero + tokens, out), reward

    def scale_weight():
        gain_load.wait()
        row = gain[...].astype(F32).reshape(1, rows) + 1.0
        column = jnp.sum(jnp.where(diagonal, row, 0.0), axis=1, keepdims=True)
        wide_gain[...] = jnp.broadcast_to(column, wide_gain.shape)
        weight_load.wait()
        w_all[pl.ds(mine, rows), :] = (weight[...].astype(F32) * column).astype(BF)

    def scale_cotangent():
        states_load.wait()

        def square_tile(i, total):
            at = pl.multiple_of(i * TILE, TILE)
            for k in range(0, TILE, 128):
                part = states[:, pl.ds(at + k, 128)].astype(F32)
                total = total + part * part
            return total

        squares = lax.fori_loop(0, tiles, square_tile, jnp.zeros((seq, 128), F32))
        inverse[...] = lax.rsqrt(jnp.sum(squares, axis=1, keepdims=True) / width + EPSILON)
        cot_load.wait()
        position = lax.broadcasted_iota(jnp.int32, (seq, features), 0)
        first = prompt_ref[0]
        alive = (position >= first) & (position < first + response_ref[0])
        scaled[...] = jnp.where(alive, cot[...].astype(F32) * inverse[...], 0.0).astype(BF)

    def gradient(target, after):
        def tile(begin):
            at = pl.ds(pl.multiple_of(begin, TILE), TILE)
            target[at, :] = lax.dot_general(
                states[:, at], scaled[...], (((0,), (0,)), ((), ())), preferred_element_type=F32
            ).astype(target.dtype)

        def natural(i, carry):
            tile(i * TILE)
            return carry

        aligned = rows % TILE == 0
        if not aligned:
            lax.fori_loop(0, tiles, natural, 0)
        for h in range(2):
            for m in reversed(range(count)):
                begin = pair_begin(m) + h * rows
                if aligned:
                    for k in range(0, rows, TILE):
                        tile(begin + k)
                after(m, h, pl.multiple_of(begin, rows))

    def product(m, start):
        if pair % 128:
            return
        at = pl.ds(pair_begin(m), pair)
        value = jnp.dot(states[:, at], w_all[at, :], preferred_element_type=F32)
        acc[...] = value if start else acc[...] + value

    def key_values():
        if pair % 128:
            acc[...] = jnp.dot(states[...], w_all[...], preferred_element_type=F32)
        kv_ref[0] = jnp.where(inverse[...] > 0.0, acc[...] * inverse[...], 0.0).astype(BF)

    def last(order, m):
        return max(i for i in range(bits) if (m >> order[i]) & 1)

    def w_copy(p, m, h):
        bit = orders[p][last(orders[p], m)]
        at = pl.ds(pl.multiple_of(pair_begin(m ^ (1 << bit)) + h * rows, rows), rows)
        ref = w_all.at[at, pl.ds(p * half, half)]
        i = (p * count + m) * 2 + h
        return remote(ref, ref, w_send.at[i], w_recv.at[i], across(bit))

    def fw_copy(p, m, h):
        at = pl.ds(pl.multiple_of(pair_begin(m) + h * rows, rows), rows)
        ref = w_all.at[at, pl.ds(p * half, half)]
        i = (p * count + m) * 2 + h
        return remote(ref, ref, fw_send.at[i], fw_recv.at[i], partner)

    def odd_copy():
        at = pl.ds(pl.multiple_of(j * pair + rows, rows), rows)
        ref = w_all.at[at, :]
        return remote(ref, ref, fw_send.at[1], fw_recv.at[1], partner)

    def g_copy(m, h, begin):
        i = m * 2 + h
        return remote(
            grad_send.at[pl.ds(begin, rows)], grad_in.at[m, pl.ds(h * rows, rows)],
            g_send.at[i], g_recv.at[i], partner,
        )

    def fin_copy(c):
        return remote(fin_out.at[c], fin_in.at[c], fin_send.at[c], fin_recv.at[c], partner)

    def pair_scalars():
        return remote(scal_pair.at[0], scal_pair.at[1], s_send.at[0], s_recv.at[0], partner)

    def finished(total, c):
        at = slice((c % (chunks // 2)) * chunk_rows, (c % (chunks // 2) + 1) * chunk_rows)
        column = wide_gain[at, 0:1]
        gw_ref[at, :] = total * column
        gcol[at, :] = jnp.sum(total * weight[at, :].astype(F32), axis=1, keepdims=True)

    def grad_gain():
        gg_ref[...] = jnp.sum(jnp.where(diagonal, gcol[...], 0.0), axis=0, keepdims=True)

    levels = [[m for m in range(count) if m.bit_count() == n] for n in range(bits + 1)]

    @pl.when(jnp.logical_not(odd))
    def _():
        pl.semaphore_wait(barrier, bits + 1)
        scal, _ = scalars()
        scal_pair[0] = scal
        launch(pair_scalars())
        scale_weight()
        for s in range(bits):
            for p in range(2):
                launch(w_copy(p, 1 << orders[p][s], 0))
        scale_cotangent()
        gradient(grad_send, lambda m, h, begin: launch(g_copy(m, h, begin)))
        odd_copy().wait_recv()
        for s in range(bits):
            for p in range(2):
                launch(w_copy(p, 1 << orders[p][s], 1))
        for p in range(2):
            launch(fw_copy(p, 0, 0))
        product(0, True)
        for n in range(1, bits + 1):
            for m in levels[n]:
                for p in range(2):
                    for h in range(2):
                        w_copy(p, m, h).wait_recv()
                        launch(fw_copy(p, m, h))
            if n == 1:
                pl.semaphore_wait(gate, 1)
            for m in levels[n]:
                for p in range(2):
                    for s in range(last(orders[p], m) + 1, bits):
                        for h in range(2):
                            launch(w_copy(p, m | (1 << orders[p][s]), h))
            for m in levels[n]:
                product(m, False)
        key_values()
        for c in range(chunks // 2):
            fin_copy(c).wait_recv()
            finished(fin_in[c], c)
        grad_gain()
        finish()

    @pl.when(odd)
    def _():
        pl.semaphore_wait(barrier, len(peers) + 1)
        scal, reward = scalars()
        pair_scalars().wait_recv()
        low = scal_pair[1]
        total = scal + low
        slot = 0

        def exchange(stage, slot):
            copies = []
            for k, m in stage:
                copies.append(launch(remote(
                    scal_out.at[which], scal_in.at[slot], s_send.at[1 + slot], s_recv.at[1 + slot],
                    peer(k, m),
                )))
                slot += 1
            return copies, slot

        def collect(total, copies, slot):
            for copy in copies:
                copy.wait_recv()
            for i in range(slot - len(copies), slot):
                total = total + scal_in[i]
            return total

        which = 0
        scal_out[0] = total
        copies, slot = exchange(stages[0], slot)
        scale_weight()
        launch(odd_copy())
        scale_cotangent()
        gradient(grad, lambda m, h, begin: None)
        total = collect(total, copies, slot)
        for which in range(1, len(stages)):
            scal_out[which] = total
            copies, slot = exchange(stages[which], slot)
            total = collect(total, copies, slot)

        def pick(source, index):
            return jnp.sum(jnp.where(lane == index, source, 0.0), axis=1, keepdims=True)

        number = float(R * F)
        average = pick(total, 0) / number
        variance = pick(total, 1) / number - average * average
        size = lax.rsqrt(variance + EPSILON) * lax.rsqrt(pick(total, 2))
        coef = (reward - average) * size
        coef_low = (pick(low, 0) - average) * size

        starts = [count - (count >> i) for i in range(bits + 1)]
        arrived = set()

        def chunk_at(c):
            return pl.ds(c * chunk_rows, chunk_rows)

        def partial(p, q, c, step):
            m = offset_of(q, orders[p])
            h = c // (chunks // 2)
            if (m, h) not in arrived:
                arrived.add((m, h))
                g_copy(m, h, pl.multiple_of(pair_begin(m) + h * rows, rows)).wait_recv()
            columns = slice(p * half, (p + 1) * half)
            begin = pl.multiple_of(pair_begin(m) + c * chunk_rows, chunk_rows)
            value = grad[pl.ds(begin, chunk_rows), columns] * coef
            value = value + grad_in[m, chunk_at(c), columns].astype(F32) * coef_low
            for i in range(step):
                x_copy(p, i, q, c).wait_recv()
                value = value + receiving[p, starts[i] + q, chunk_at(c)].astype(F32)
            return value

        def x_copy(p, step, q, c):
            i = (p * (count - 1) + starts[step] + q) * chunks + c
            return remote(
                sending.at[p, starts[step] + q, chunk_at(c)],
                receiving.at[p, starts[step] + q, chunk_at(c)],
                x_send.at[i], x_recv.at[i], across(orders[p][step]),
            )

        def scatter(step, q, c):
            keep = count >> (step + 1)
            for p in range(2):
                sending[p, starts[step] + q, chunk_at(c)] = partial(p, keep + q, c, step).astype(BF)
                launch(x_copy(p, step, q, c))

        def z_copy(way, c):
            after = r + 1 - 2 * way
            return remote(
                chain_out.at[way, c], chain_in.at[way, c],
                z_send.at[way * chunks + c], z_recv.at[way * chunks + c],
                (lax.rem(after + R, R), f),
            )

        def place(way):
            return r if way == 0 else R - 1 - r

        def gather_own(c):
            for p in range(2):
                own[c, :, p * half:(p + 1) * half] = partial(p, 0, c, bits)

        def relay(hop, c):
            for way in range(2):
                @pl.when(place(way) == hop)
                def _(way=way):
                    value = own[c]
                    if hop:
                        z_copy(way, c).wait_recv()
                        value = value + chain_in[way, c].astype(F32)
                    chain_out[way, c] = value.astype(chain_out.dtype)
                    z_copy(way, c).start()

        def total_of(c):
            for way in range(2):
                @pl.when(place(way) == R - 1)
                def _(way=way):
                    z_copy(way, c).wait_recv()
            value = own[c]
            for way in range(2):
                value = value + jnp.where(place(way) > 0, chain_in[way, c].astype(F32), 0.0)
            if c < chunks // 2:
                fin_out[c] = value
                launch(fin_copy(c))
            else:
                finished(value, c)

        def products(n):
            for m in levels[n]:
                for p in range(2):
                    for h in range(2 if m else 1):
                        fw_copy(p, m, h).wait_recv()
                product(m, m == 0)

        def open_gate():
            pl.semaphore_signal(gate, inc=1, device_id=partner, device_id_type=MESH)

        events = []

        def at(key, action, *arguments):
            events.append((key, len(events), action, arguments))

        period = count - 1
        final = HOP * bits
        for c in range(chunks):
            for step in range(bits):
                keep = count >> (step + 1)
                for q in reversed(range(keep)):
                    late = 0 if 2 * q >= keep and keep > 1 else HOP - 2
                    if step == bits - 1:
                        late = 0
                    at(period * c + HOP * step + late, scatter, step, q, c)
            at(period * c + final, gather_own, c)
            for hop in range(R - 1):
                at(period * c + final + HOP * hop, relay, hop, c)
            at(period * c + final + HOP * (R - 1), total_of, c)
        ending = period * (chunks - 1) + final
        at(ending - HOP // 2, open_gate)
        at(ending - HOP, products, 0)
        for n in range(1, bits + 1):
            at(ending + n if n < bits else ending + HOP * (R - 2) + 1, products, n)
        at(ending + HOP * (R - 2) + 2, key_values)
        for _, _, action, arguments in sorted(events, key=lambda e: e[:2]):
            action(*arguments)
        grad_gain()
        finish()
        for way in range(2):
            @pl.when(place(way) < R - 1)
            def _(way=way):
                for c in range(chunks):
                    z_copy(way, c).wait_send()


def shards(R, F, states, cotangent, kv_weight, norm_gain, prompt_len, response_len, reward_bucket):
    _, seq, width = states.shape
    rows, features = kv_weight.shape
    half = features // 2
    bits, count, stages = plan(R, F)
    pair = 2 * rows
    chunk_rows = max(pair // 8, 16)
    chunks = pair // chunk_rows
    wire = BF if R <= 4 else F32
    slots = sum(len(stage) for stage in stages)
    vmem = pl.BlockSpec(memory_space=pltpu.VMEM)
    hbm = pl.BlockSpec(memory_space=pltpu.HBM)
    smem = pl.BlockSpec(memory_space=pltpu.SMEM)
    dma = pltpu.SemaphoreType.DMA
    key_values, grad_weight, grad_gain = pl.pallas_call(
        functools.partial(kernel, R, F, chunk_rows),
        out_shape=(
            jax.ShapeDtypeStruct((1, seq, features), BF),
            jax.ShapeDtypeStruct((rows, features), F32),
            jax.ShapeDtypeStruct((1, rows), F32),
        ),
        in_specs=[hbm] * 4 + [smem] * 3,
        out_specs=(vmem, vmem, vmem),
        scratch_shapes=[
            pltpu.VMEM((seq, width), BF),
            pltpu.VMEM((seq, features), BF),
            pltpu.VMEM((seq, features), BF),
            pltpu.VMEM((rows, features), BF),
            pltpu.VMEM((width, features), BF),
            pltpu.VMEM((rows,), BF),
            pltpu.VMEM((width, features), F32),
            pltpu.VMEM((width, features), BF),
            pltpu.VMEM((count, pair, features), BF),
            pltpu.VMEM((2, max(count - 1, 1), pair, half), BF),
            pltpu.VMEM((2, max(count - 1, 1), pair, half), BF),
            pltpu.VMEM((chunks, chunk_rows, features), F32),
            pltpu.VMEM((2, chunks, chunk_rows, features), wire),
            pltpu.VMEM((2, chunks, chunk_rows, features), wire),
            pltpu.VMEM((chunks // 2, chunk_rows, features), F32),
            pltpu.VMEM((chunks // 2, chunk_rows, features), F32),
            pltpu.VMEM((len(stages), 1, 128), F32),
            pltpu.VMEM((2, 1, 128), F32),
            pltpu.VMEM((slots, 1, 128), F32),
            pltpu.VMEM((seq, features), F32),
            pltpu.VMEM((seq, 1), F32),
            pltpu.VMEM((rows, 1), F32),
            pltpu.VMEM((rows, 128), F32),
            dma((4,)),
            dma((4 * count,)), dma((4 * count,)),
            dma((4 * count,)), dma((4 * count,)),
            dma((2 * count,)), dma((2 * count,)),
            dma((2 * count * chunks,)), dma((2 * count * chunks,)),
            dma((2 * chunks,)), dma((2 * chunks,)),
            dma((chunks // 2,)), dma((chunks // 2,)),
            dma((1 + slots,)), dma((1 + slots,)),
            pltpu.SemaphoreType.REGULAR,
        ],
        compiler_params=pltpu.CompilerParams(
            collective_id=0, has_side_effects=True, vmem_limit_bytes=40 * 1024 * 1024
        ),
    )(
        *[
            pltpu.with_memory_space_constraint(x, pltpu.HBM)
            for x in (states, cotangent, kv_weight, norm_gain)
        ],
        prompt_len, response_len, reward_bucket,
    )
    return key_values, grad_weight, grad_gain.reshape(rows)


def solution(mesh):
    placed = (
        P(("replica", "fsdp"), None, None),
        P(("replica", "fsdp"), None, None),
        P("fsdp", None),
        P("fsdp"),
        P(("replica", "fsdp")),
        P(("replica", "fsdp")),
        P(("replica", "fsdp")),
    )
    return jax.shard_map(
        functools.partial(shards, mesh.shape["replica"], mesh.shape["fsdp"]),
        mesh=mesh,
        in_specs=placed,
        out_specs=(P(("replica", "fsdp"), None, None), P("fsdp", None), P("fsdp")),
        check_vma=False,
    )
```

time: 51.9 us -> 36.9 us (0.71)
  the two profiles are of different devices: /device:TPU:0 before, /device:TPU:1 now
where the time goes in v1:
time: 36.9 us; the launch traced here: 36.7 us
  Pallas kernels  32.1 us (87%)
  between operations  2.58 us (7%)
  local copies, waits for them, and re-layouts  2.06 us (6%)
    pallas_call x1, Pallas kernels, shards(): pl.pallas_call(functools.partial(kernel, R, F, chunk_rows), out_shape=(ja...  32.1 us
    unnamed x3, local copies, waits for them, and re-layouts  2.06 us

profile of v1, /device:TPU:1, one launch (start us, length us, event | category | flops | bytes accessed | tf_op | source)
XLA Modules:
  0.0 36.7 jit_solution(4400033773900649847)
XLA Ops:
  2.6 32.1 %shard_map.94 = (bf16[1,256,512]{2,1,0:T(8,128)(2,1)S(1)}, f32[256,512]{1,0:T(8,128)S(1)}, f32[1,256]{1,0:T(1,128)S(1)}) custom-call(bf16[1,256,2048]{2,1,0:T(8,128)(2,1)} %states_hbm.1, bf16[1,256,512]{2,1,0:T(8,128)(2,1)} %cot_hbm.1, bf16[256,512]{1,0:T(8,128)(2,1)} %weight_hbm.1, bf16[256]{0:T(256)(128)(2,1)} %gain_hbm.1, s32[1]{0:T(128)S(6)} %copy.13.prompt_ref, ...), custom_call_target="tpu_custom_call" | custom-call | tf_op jit(solution)/shard_map/pallas_call | solution.py:463
  34.6 0.7 %copy.16 = bf16[1,256,512]{2,1,0:T(8,128)(2,1)} copy(bf16[1,256,512]{2,1,0:T(8,128)(2,1)S(1)} %get-tuple-element.12) | data formatting | bytes 524288
  35.3 0.8 %copy.17 = f32[256,512]{1,0:T(8,128)} copy(f32[256,512]{1,0:T(8,128)S(1)} %get-tuple-element.13) | data formatting | bytes 1048576
  36.1 0.6 %copy.18 = f32[256]{0:T(256)} copy(f32[256]{0:T(256)S(1)} %bitcast.1) | data formatting | bytes 2048

commit v2 on v1

--- a/solution.py
+++ b/solution.py
@@ -12,6 +12,7 @@
 BF = jnp.bfloat16
 F32 = jnp.float32
 TILE = 256
+LAG = 11
 HOP = 8
 
 
@@ -49,8 +50,7 @@
     states, cot, scaled, weight, w_all, gain,
     grad, grad_send, grad_in, sending, receiving, own, chain_out, chain_in,
     fin_out, fin_in, scal_out, scal_pair, scal_in, acc, inverse, gcol, wide_gain,
-    load_sem, w_send, w_recv, fw_send, fw_recv, g_send, g_recv, x_send, x_recv,
-    z_send, z_recv, fin_send, fin_recv, s_send, s_recv, gate,
+    load_sem, send_sem, w_recv, fw_recv, g_recv, x_recv, z_recv, fin_recv, s_recv, gate,
 ):
     r, f = lax.axis_index("replica"), lax.axis_index("fsdp")
     bits, count, stages = plan(R, F)
@@ -65,7 +65,6 @@
     tiles = width // TILE
     chunks = pair // chunk_rows
     partner = (r, flip(f, 1))
-    pending = []
 
     def remote(src, dst, send_sem, recv_sem, device):
         return pltpu.make_async_remote_copy(
@@ -73,15 +72,11 @@
             device_id=device, device_id_type=MESH,
         )
 
-    def launch(copy):
-        copy.start()
-        pending.append(copy)
-        return copy
-
-    def finish():
-        for copy in pending:
-            copy.wait_send()
-        pending.clear()
+    def sent(ref, send_sem):
+        remote(ref, ref, send_sem, send_sem, partner).wait_send()
+
+    def got(ref, recv_sem):
+        remote(ref, ref, recv_sem, recv_sem, partner).wait_recv()
 
     def across(bit):
         return (r, flip(f, 2 << bit))
@@ -193,36 +188,44 @@
     def last(order, m):
         return max(i for i in range(bits) if (m >> order[i]) & 1)
 
+    def w_rows(m, h):
+        return pl.ds(pl.multiple_of(pair_begin(m) + h * rows, rows), rows)
+
     def w_copy(p, m, h):
         bit = orders[p][last(orders[p], m)]
-        at = pl.ds(pl.multiple_of(pair_begin(m ^ (1 << bit)) + h * rows, rows), rows)
-        ref = w_all.at[at, pl.ds(p * half, half)]
-        i = (p * count + m) * 2 + h
-        return remote(ref, ref, w_send.at[i], w_recv.at[i], across(bit))
-
-    def fw_copy(p, m, h):
-        at = pl.ds(pl.multiple_of(pair_begin(m) + h * rows, rows), rows)
-        ref = w_all.at[at, pl.ds(p * half, half)]
-        i = (p * count + m) * 2 + h
-        return remote(ref, ref, fw_send.at[i], fw_recv.at[i], partner)
-
-    def odd_copy():
-        at = pl.ds(pl.multiple_of(j * pair + rows, rows), rows)
-        ref = w_all.at[at, :]
-        return remote(ref, ref, fw_send.at[1], fw_recv.at[1], partner)
+        ref = w_all.at[w_rows(m ^ (1 << bit), h), pl.ds(p * half, half)]
+        return remote(ref, ref, send_sem.at[0], w_recv.at[p * count + m], across(bit))
+
+    def hand(p, m, h):
+        ref = w_all.at[w_rows(m, h), pl.ds(p * half, half)]
+        remote(ref, ref, send_sem.at[1], fw_recv.at[m], partner).start()
+
+    def handed(m, h):
+        got(w_all.at[w_rows(m, h)], fw_recv.at[m])
+
+    def received(p, m, h):
+        w_copy(p, m, h).wait_recv()
+        hand(p, m, h)
+
+    def forward(p, m, h):
+        for s in range(last(orders[p], m) + 1, bits):
+            w_copy(p, m | (1 << orders[p][s]), h).start()
 
     def g_copy(m, h, begin):
-        i = m * 2 + h
         return remote(
             grad_send.at[pl.ds(begin, rows)], grad_in.at[m, pl.ds(h * rows, rows)],
-            g_send.at[i], g_recv.at[i], partner,
+            send_sem.at[2], g_recv.at[m * 2 + h], partner,
         )
 
     def fin_copy(c):
-        return remote(fin_out.at[c], fin_in.at[c], fin_send.at[c], fin_recv.at[c], partner)
+        return remote(fin_out.at[c], fin_in.at[c], send_sem.at[2], fin_recv.at[c], partner)
 
     def pair_scalars():
-        return remote(scal_pair.at[0], scal_pair.at[1], s_send.at[0], s_recv.at[0], partner)
+        return remote(scal_pair.at[0], scal_pair.at[1], send_sem.at[3], s_recv.at[0], partner)
+
+    def finish_weight():
+        sent(w_all.at[pl.ds(0, (count - 1) * rows)], send_sem.at[0])
+        sent(w_all.at[pl.ds(0, count * rows)], send_sem.at[1])
 
     def finished(total, c):
         at = slice((c % (chunks // 2)) * chunk_rows, (c % (chunks // 2) + 1) * chunk_rows)
@@ -234,47 +237,46 @@
         gg_ref[...] = jnp.sum(jnp.where(diagonal, gcol[...], 0.0), axis=0, keepdims=True)
 
     levels = [[m for m in range(count) if m.bit_count() == n] for n in range(bits + 1)]
+    firsts = [(p, 1 << orders[p][0]) for p in range(2)]
 
     @pl.when(jnp.logical_not(odd))
     def _():
         pl.semaphore_wait(barrier, bits + 1)
         scal, _ = scalars()
         scal_pair[0] = scal
-        launch(pair_scalars())
+        pair_scalars().start()
         scale_weight()
         for s in range(bits):
             for p in range(2):
-                launch(w_copy(p, 1 << orders[p][s], 0))
+                w_copy(p, 1 << orders[p][s], 0).start()
         scale_cotangent()
-        gradient(grad_send, lambda m, h, begin: launch(g_copy(m, h, begin)))
-        odd_copy().wait_recv()
-        for s in range(bits):
+        gradient(grad_send, lambda m, h, begin: g_copy(m, h, begin).start())
+        for p in range(2):
+            hand(p, 0, 0)
+        handed(0, 1)
+        product(0, True)
+        for m in levels[1]:
             for p in range(2):
-                launch(w_copy(p, 1 << orders[p][s], 1))
-        for p in range(2):
-            launch(fw_copy(p, 0, 0))
-        product(0, True)
+                received(p, m, 0)
+        pl.semaphore_wait(gate, 1)
         for n in range(1, bits + 1):
             for m in levels[n]:
                 for p in range(2):
-                    for h in range(2):
-                        w_copy(p, m, h).wait_recv()
-                        launch(fw_copy(p, m, h))
-            if n == 1:
-                pl.semaphore_wait(gate, 1)
+                    if n > 1:
+                        received(p, m, 0)
+                    forward(p, m, 0)
+        for n in range(1, bits + 1):
             for m in levels[n]:
-                for p in range(2):
-                    for s in range(last(orders[p], m) + 1, bits):
-                        for h in range(2):
-                            launch(w_copy(p, m | (1 << orders[p][s]), h))
-            for m in levels[n]:
+                handed(m, 1)
                 product(m, False)
         key_values()
         for c in range(chunks // 2):
             fin_copy(c).wait_recv()
             finished(fin_in[c], c)
         grad_gain()
-        finish()
+        finish_weight()
+        sent(grad_send, send_sem.at[2])
+        sent(scal_pair.at[0], send_sem.at[3])
 
     @pl.when(odd)
     def _():
@@ -283,37 +285,36 @@
         pair_scalars().wait_recv()
         low = scal_pair[1]
         total = scal + low
-        slot = 0
-
-        def exchange(stage, slot):
-            copies = []
-            for k, m in stage:
-                copies.append(launch(remote(
-                    scal_out.at[which], scal_in.at[slot], s_send.at[1 + slot], s_recv.at[1 + slot],
-                    peer(k, m),
-                )))
-                slot += 1
-            return copies, slot
-
-        def collect(total, copies, slot):
-            for copy in copies:
-                copy.wait_recv()
-            for i in range(slot - len(copies), slot):
+
+        def exchange(which, total):
+            first = sum(len(stage) for stage in stages[:which])
+            scal_out[which] = total
+            for i, (k, m) in enumerate(stages[which]):
+                remote(
+                    scal_out.at[which], scal_in.at[first + i], send_sem.at[3],
+                    s_recv.at[1 + which], peer(k, m),
+                ).start()
+
+        def collect(which, total):
+            first = sum(len(stage) for stage in stages[:which])
+            size = len(stages[which])
+            got(scal_in.at[pl.ds(first, size)], s_recv.at[1 + which])
+            for i in range(first, first + size):
                 total = total + scal_in[i]
             return total
 
-        which = 0
-        scal_out[0] = total
-        copies, slot = exchange(stages[0], slot)
+        exchange(0, total)
         scale_weight()
-        launch(odd_copy())
+        for p, m in firsts:
+            w_copy(p, m, 1).start()
+        for p in range(2):
+            hand(p, 0, 1)
         scale_cotangent()
         gradient(grad, lambda m, h, begin: None)
-        total = collect(total, copies, slot)
+        total = collect(0, total)
         for which in range(1, len(stages)):
-            scal_out[which] = total
-            copies, slot = exchange(stages[which], slot)
-            total = collect(total, copies, slot)
+            exchange(which, total)
+            total = collect(which, total)
 
         def pick(source, index):
             return jnp.sum(jnp.where(lane == index, source, 0.0), axis=1, keepdims=True)
@@ -331,40 +332,43 @@
         def chunk_at(c):
             return pl.ds(c * chunk_rows, chunk_rows)
 
+        def arrive(q, c, step):
+            for p in range(2):
+                m, h = offset_of(q, orders[p]), c // (chunks // 2)
+                if (m, h) not in arrived:
+                    arrived.add((m, h))
+                    g_copy(m, h, w_rows(m, h).start).wait_recv()
+            for i in range(step):
+                slot = starts[i] + q
+                got(receiving.at[:, slot, chunk_at(c)], x_recv.at[slot * chunks + c])
+
         def partial(p, q, c, step):
             m = offset_of(q, orders[p])
-            h = c // (chunks // 2)
-            if (m, h) not in arrived:
-                arrived.add((m, h))
-                g_copy(m, h, pl.multiple_of(pair_begin(m) + h * rows, rows)).wait_recv()
             columns = slice(p * half, (p + 1) * half)
             begin = pl.multiple_of(pair_begin(m) + c * chunk_rows, chunk_rows)
             value = grad[pl.ds(begin, chunk_rows), columns] * coef
             value = value + grad_in[m, chunk_at(c), columns].astype(F32) * coef_low
             for i in range(step):
-                x_copy(p, i, q, c).wait_recv()
                 value = value + receiving[p, starts[i] + q, chunk_at(c)].astype(F32)
             return value
 
-        def x_copy(p, step, q, c):
-            i = (p * (count - 1) + starts[step] + q) * chunks + c
-            return remote(
-                sending.at[p, starts[step] + q, chunk_at(c)],
-                receiving.at[p, starts[step] + q, chunk_at(c)],
-                x_send.at[i], x_recv.at[i], across(orders[p][step]),
-            )
-
         def scatter(step, q, c):
             keep = count >> (step + 1)
+            slot = starts[step] + q
+            arrive(keep + q, c, step)
             for p in range(2):
-                sending[p, starts[step] + q, chunk_at(c)] = partial(p, keep + q, c, step).astype(BF)
-                launch(x_copy(p, step, q, c))
-
-        def z_copy(way, c):
+                sending[p, slot, chunk_at(c)] = partial(p, keep + q, c, step).astype(BF)
+                remote(
+                    sending.at[p, slot, chunk_at(c)], receiving.at[p, slot, chunk_at(c)],
+                    send_sem.at[4], x_recv.at[slot * chunks + c], across(orders[p][step]),
+                ).start()
+
+        def z_copy(way, c, p):
             after = r + 1 - 2 * way
+            columns = pl.ds(p * half, half)
             return remote(
-                chain_out.at[way, c], chain_in.at[way, c],
-                z_send.at[way * chunks + c], z_recv.at[way * chunks + c],
+                chain_out.at[way, c, :, columns], chain_in.at[way, c, :, columns],
+                send_sem.at[5 + way], z_recv.at[(way * chunks + c) * 2 + p],
                 (lax.rem(after + R, R), f),
             )
 
@@ -372,6 +376,7 @@
             return r if way == 0 else R - 1 - r
 
         def gather_own(c):
+            arrive(0, c, bits)
             for p in range(2):
                 own[c, :, p * half:(p + 1) * half] = partial(p, 0, c, bits)
 
@@ -379,71 +384,94 @@
             for way in range(2):
                 @pl.when(place(way) == hop)
                 def _(way=way):
-                    value = own[c]
-                    if hop:
-                        z_copy(way, c).wait_recv()
-                        value = value + chain_in[way, c].astype(F32)
-                    chain_out[way, c] = value.astype(chain_out.dtype)
-                    z_copy(way, c).start()
+                    for p in range(2):
+                        columns = slice(p * half, (p + 1) * half)
+                        value = own[c, :, columns]
+                        if hop:
+                            z_copy(way, c, p).wait_recv()
+                            value = value + chain_in[way, c, :, columns].astype(F32)
+                        chain_out[way, c, :, columns] = value.astype(chain_out.dtype)
+                        z_copy(way, c, p).start()
 
         def total_of(c):
             for way in range(2):
                 @pl.when(place(way) == R - 1)
                 def _(way=way):
-                    z_copy(way, c).wait_recv()
+                    for p in range(2):
+                        z_copy(way, c, p).wait_recv()
             value = own[c]
             for way in range(2):
                 value = value + jnp.where(place(way) > 0, chain_in[way, c].astype(F32), 0.0)
             if c < chunks // 2:
                 fin_out[c] = value
-                launch(fin_copy(c))
+                fin_copy(c).start()
             else:
                 finished(value, c)
 
         def products(n):
             for m in levels[n]:
-                for p in range(2):
-                    for h in range(2 if m else 1):
-                        fw_copy(p, m, h).wait_recv()
+                handed(m, 0)
                 product(m, m == 0)
 
         def open_gate():
             pl.semaphore_signal(gate, inc=1, device_id=partner, device_id_type=MESH)
 
+        def weight_first():
+            for p, m in firsts:
+                received(p, m, 1)
+
+        def weight_second():
+            for p, m in firsts:
+                for s in range(1, bits):
+                    w_copy(p, 1 << orders[p][s], 1).start()
+                forward(p, m, 1)
+
+        def weight_level(n):
+            for m in levels[n]:
+                for p in range(2):
+                    if (p, m) not in firsts:
+                        received(p, m, 1)
+                        forward(p, m, 1)
+
         events = []
 
         def at(key, action, *arguments):
             events.append((key, len(events), action, arguments))
 
         period = count - 1
-        final = HOP * bits
+        final = LAG * bits
         for c in range(chunks):
             for step in range(bits):
                 keep = count >> (step + 1)
                 for q in reversed(range(keep)):
-                    late = 0 if 2 * q >= keep and keep > 1 else HOP - 2
-                    if step == bits - 1:
-                        late = 0
-                    at(period * c + HOP * step + late, scatter, step, q, c)
+                    late = 6 if 2 * q < keep and step < bits - 1 else 0
+                    at(period * c + LAG * step + late, scatter, step, q, c)
             at(period * c + final, gather_own, c)
             for hop in range(R - 1):
                 at(period * c + final + HOP * hop, relay, hop, c)
             at(period * c + final + HOP * (R - 1), total_of, c)
-        ending = period * (chunks - 1) + final
-        at(ending - HOP // 2, open_gate)
-        at(ending - HOP, products, 0)
+        scattered = period * (chunks - 1) + LAG * (bits - 1)
+        ending = period * (chunks - 1) + final + HOP * (R - 1)
+        at(final, weight_first)
+        at(final, products, 0)
+        at(scattered, weight_second)
+        at(scattered + 5, open_gate)
         for n in range(1, bits + 1):
-            at(ending + n if n < bits else ending + HOP * (R - 2) + 1, products, n)
-        at(ending + HOP * (R - 2) + 2, key_values)
+            late = (bits - n) * HOP
+            at(ending - 14 - late, weight_level, n)
+            at(ending - 9 - late, products, n)
+        at(ending - 9, key_values)
         for _, _, action, arguments in sorted(events, key=lambda e: e[:2]):
             action(*arguments)
         grad_gain()
-        finish()
+        finish_weight()
+        sent(fin_out, send_sem.at[2])
+        sent(scal_in, send_sem.at[3])
+        sent(sending, send_sem.at[4])
         for way in range(2):
             @pl.when(place(way) < R - 1)
             def _(way=way):
-                for c in range(chunks):
-                    z_copy(way, c).wait_send()
+                sent(chain_out.at[way], send_sem.at[5 + way])
 
 
 def shards(R, F, states, cotangent, kv_weight, norm_gain, prompt_len, response_len, reward_bucket):
@@ -494,13 +522,14 @@
             pltpu.VMEM((rows, 1), F32),
             pltpu.VMEM((rows, 128), F32),
             dma((4,)),
-            dma((4 * count,)), dma((4 * count,)),
-            dma((4 * count,)), dma((4 * count,)),
-            dma((2 * count,)), dma((2 * count,)),
-            dma((2 * count * chunks,)), dma((2 * count * chunks,)),
-            dma((2 * chunks,)), dma((2 * chunks,)),
-            dma((chunks // 2,)), dma((chunks // 2,)),
-            dma((1 + slots,)), dma((1 + slots,)),
+            dma((7,)),
+            dma((2 * count,)),
+            dma((count,)),
+            dma((2 * count,)),
+            dma((max(count - 1, 1) * chunks,)),
+            dma((4 * chunks,)),
+            dma((chunks // 2,)),
+            dma((1 + len(stages),)),
             pltpu.SemaphoreType.REGULAR,
         ],
         compiler_params=pltpu.CompilerParams(

time: 36.9 us -> 33.7 us (0.913)
  Pallas kernels: 32.1 us -> 28.9 us
    pallas_call x1, Pallas kernels: 32.1 us -> 28.9 us  [shards(): pl.pallas_call(functools.partial(kernel, R, F, chunk_rows), out_shape=(ja...]
where the time goes in v2:
time: 33.7 us; the launch traced here: 33.5 us
  Pallas kernels  28.9 us (86%)
  between operations  2.58 us (8%)
  local copies, waits for them, and re-layouts  2.06 us (6%)
    pallas_call x1, Pallas kernels, shards(): pl.pallas_call(functools.partial(kernel, R, F, chunk_rows), out_shape=(ja...  28.9 us
    unnamed x3, local copies, waits for them, and re-layouts  2.06 us

profile of v2, /device:TPU:1, one launch (start us, length us, event | category | flops | bytes accessed | tf_op | source)
XLA Modules:
  0.0 33.5 jit_solution(7874702470543000466)
XLA Ops:
  2.6 28.9 %shard_map.94 = (bf16[1,256,512]{2,1,0:T(8,128)(2,1)S(1)}, f32[256,512]{1,0:T(8,128)S(1)}, f32[1,256]{1,0:T(1,128)S(1)}) custom-call(bf16[1,256,2048]{2,1,0:T(8,128)(2,1)} %states_hbm.1, bf16[1,256,512]{2,1,0:T(8,128)(2,1)} %cot_hbm.1, bf16[256,512]{1,0:T(8,128)(2,1)} %weight_hbm.1, bf16[256]{0:T(256)(128)(2,1)} %gain_hbm.1, s32[1]{0:T(128)S(6)} %copy.13.prompt_ref, ...), custom_call_target="tpu_custom_call" | custom-call | tf_op jit(solution)/shard_map/pallas_call | solution.py:491
  31.5 0.7 %copy.16 = bf16[1,256,512]{2,1,0:T(8,128)(2,1)} copy(bf16[1,256,512]{2,1,0:T(8,128)(2,1)S(1)} %get-tuple-element.12) | data formatting | bytes 524288
  32.2 0.8 %copy.17 = f32[256,512]{1,0:T(8,128)} copy(f32[256,512]{1,0:T(8,128)S(1)} %get-tuple-element.13) | data formatting | bytes 1048576
  33.0 0.6 %copy.18 = f32[256]{0:T(256)} copy(f32[256]{0:T(256)S(1)} %bitcast.1) | data formatting | bytes 2048

commit v3 on v2

--- a/solution.py
+++ b/solution.py
@@ -459,8 +459,8 @@
         for n in range(1, bits + 1):
             late = (bits - n) * HOP
             at(ending - 14 - late, weight_level, n)
-            at(ending - 9 - late, products, n)
-        at(ending - 9, key_values)
+            at(ending - 7 - late, products, n)
+        at(ending - 7, key_values)
         for _, _, action, arguments in sorted(events, key=lambda e: e[:2]):
             action(*arguments)
         grad_gain()
@@ -472,6 +472,18 @@
             @pl.when(place(way) < R - 1)
             def _(way=way):
                 sent(chain_out.at[way], send_sem.at[5 + way])
+
+
+def writer(*refs):
+    *pairs, sem = refs
+    copies = [
+        pltpu.make_async_copy(source, target, sem.at[i])
+        for i, (source, target) in enumerate(zip(pairs[:3], pairs[3:]))
+    ]
+    for copy in copies:
+        copy.start()
+    for copy in copies:
+        copy.wait()
 
 
 def shards(R, F, states, cotangent, kv_weight, norm_gain, prompt_len, response_len, reward_bucket):
@@ -542,6 +554,20 @@
         ],
         prompt_len, response_len, reward_bucket,
     )
+    key_values, grad_weight, grad_gain = pl.pallas_call(
+        writer,
+        out_shape=(
+            jax.ShapeDtypeStruct(key_values.shape, BF),
+            jax.ShapeDtypeStruct(grad_weight.shape, F32),
+            jax.ShapeDtypeStruct(grad_gain.shape, F32),
+        ),
+        in_specs=[vmem] * 3,
+        out_specs=(hbm,) * 3,
+        scratch_shapes=[dma((3,))],
+    )(*[
+        pltpu.with_memory_space_constraint(x, pltpu.VMEM)
+        for x in (key_values, grad_weight, grad_gain)
+    ])
     return key_values, grad_weight, grad_gain.reshape(rows)
 
 

time: 33.7 us -> 31.9 us (0.947)
  local copies, waits for them, and re-layouts: 2.06 us -> 0 us
    unnamed x3 -> x0, local copies, waits for them, and re-layouts: 2.06 us -> none
    pallas_call x0 -> x1, Pallas kernels: none -> 0.91 us  [shards(): pl.pallas_call(writer, out_shape=(jax.ShapeDtypeStruct(key_values.shape,...]
    pallas_call x1, Pallas kernels: 28.9 us -> 28.2 us  [shards(): pl.pallas_call(functools.partial(kernel, R, F, chunk_rows), out_shape=(ja...]
where the time goes in v3:
time: 31.9 us; the launch traced here: 31.7 us
  Pallas kernels  29.2 us (92%)
  between operations  2.58 us (8%)
    pallas_call x1, Pallas kernels, shards(): pl.pallas_call(functools.partial(kernel, R, F, chunk_rows), out_shape=(ja...  28.2 us
    pallas_call x1, Pallas kernels, shards(): pl.pallas_call(writer, out_shape=(jax.ShapeDtypeStruct(key_values.shape,...  0.91 us

profile of v3, /device:TPU:1, one launch (start us, length us, event | category | flops | bytes accessed | tf_op | source)
XLA Modules:
  0.0 31.7 jit_solution(15900577837599614456)
XLA Ops:
  2.6 28.2 %shard_map.94 = (bf16[1,256,512]{2,1,0:T(8,128)(2,1)S(1)}, f32[256,512]{1,0:T(8,128)S(1)}, f32[1,256]{1,0:T(1,128)S(1)}) custom-call(bf16[1,256,2048]{2,1,0:T(8,128)(2,1)} %states_hbm.1, bf16[1,256,512]{2,1,0:T(8,128)(2,1)} %cot_hbm.1, bf16[256,512]{1,0:T(8,128)(2,1)} %weight_hbm.1, bf16[256]{0:T(256)(128)(2,1)} %gain_hbm.1, s32[1]{0:T(128)S(6)} %copy.10.prompt_ref, ...), custom_call_target="tpu_custom_call" | custom-call | tf_op jit(solution)/shard_map/pallas_call | solution.py:503
  30.8 0.9 %shard_map.95 = (bf16[1,256,512]{2,1,0:T(8,128)(2,1)}, f32[256,512]{1,0:T(8,128)}, f32[1,256]{1,0:T(1,128)}) custom-call(bf16[1,256,512]{2,1,0:T(8,128)(2,1)S(1)} %get-tuple-element.9.refs_0_, f32[256,512]{1,0:T(8,128)S(1)} %get-tuple-element.10.refs_1_, f32[1,256]{1,0:T(1,128)S(1)} %get-tuple-element.11.refs_2_), custom_call_target="tpu_custom_call" | custom-call | tf_op jit(solution)/shard_map/pallas_call | solution.py:557

commit v4 on v3

--- a/solution.py
+++ b/solution.py
@@ -14,6 +14,11 @@
 TILE = 256
 LAG = 11
 HOP = 8
+CAST = -5
+NEXT = 9
+ZOFF = 1
+SECOND = 0
+EARLY = 2
 
 
 def flip(me, mask):
@@ -44,13 +49,13 @@
 
 
 def kernel(
-    R, F, chunk_rows,
+    R, F, chunk_rows, early,
     states_hbm, cot_hbm, weight_hbm, gain_hbm, prompt_ref, response_ref, reward_ref,
     kv_ref, gw_ref, gg_ref,
     states, cot, scaled, weight, w_all, gain,
     grad, grad_send, grad_in, sending, receiving, own, chain_out, chain_in,
-    fin_out, fin_in, scal_out, scal_pair, scal_in, acc, inverse, gcol, wide_gain,
-    load_sem, send_sem, w_recv, fw_recv, g_recv, x_recv, z_recv, fin_recv, s_recv, gate,
+    pre_out, pre_in, cast_out, cast_in, fin_out, fin_in, scal_out, scal_pair, scal_in, acc, inverse, gcol, wide_gain,
+    load_sem, send_sem, w_recv, fw_recv, g_recv, x_recv, z_recv, pre_recv, cast_recv, fin_recv, s_recv, gate,
 ):
     r, f = lax.axis_index("replica"), lax.axis_index("fsdp")
     bits, count, stages = plan(R, F)
@@ -214,7 +219,7 @@
     def g_copy(m, h, begin):
         return remote(
             grad_send.at[pl.ds(begin, rows)], grad_in.at[m, pl.ds(h * rows, rows)],
-            send_sem.at[2], g_recv.at[m * 2 + h], partner,
+            send_sem.at[2], g_recv.at[h], partner,
         )
 
     def fin_copy(c):
@@ -227,11 +232,13 @@
         sent(w_all.at[pl.ds(0, (count - 1) * rows)], send_sem.at[0])
         sent(w_all.at[pl.ds(0, count * rows)], send_sem.at[1])
 
-    def finished(total, c):
-        at = slice((c % (chunks // 2)) * chunk_rows, (c % (chunks // 2) + 1) * chunk_rows)
-        column = wide_gain[at, 0:1]
-        gw_ref[at, :] = total * column
+    def finished(total, begin):
+        at = pl.ds(begin, total.shape[0])
+        gw_ref[at, :] = total * wide_gain[at, 0:1]
         gcol[at, :] = jnp.sum(total * weight[at, :].astype(F32), axis=1, keepdims=True)
+
+    def local(c):
+        return (c % (chunks // 2)) * chunk_rows
 
     def grad_gain():
         gg_ref[...] = jnp.sum(jnp.where(diagonal, gcol[...], 0.0), axis=0, keepdims=True)
@@ -272,7 +279,7 @@
         key_values()
         for c in range(chunks // 2):
             fin_copy(c).wait_recv()
-            finished(fin_in[c], c)
+            finished(fin_in[c], local(c))
         grad_gain()
         finish_weight()
         sent(grad_send, send_sem.at[2])
@@ -327,27 +334,59 @@
         coef_low = (pick(low, 0) - average) * size
 
         starts = [count - (count >> i) for i in range(bits + 1)]
-        arrived = set()
+        arrived, halves = set(), set()
+
+        part = chunk_rows // 2
+        rounds = R.bit_length() - 1
+        side = lax.rem(r, 2)
+
+        def height(c):
+            return part if c < early else chunk_rows
 
         def chunk_at(c):
-            return pl.ds(c * chunk_rows, chunk_rows)
+            return pl.ds(c * chunk_rows, height(c))
+
+        def need(m, h):
+            if h not in halves:
+                halves.add(h)
+                got(grad_in.at[:, pl.ds(h * rows, rows)], g_recv.at[h])
+
+        def scaled_rows(m, begin, size, columns):
+            at = pl.ds(pl.multiple_of(pair_begin(m) + begin, size), size)
+            value = grad[at, columns] * coef
+            at = pl.ds(pl.multiple_of(begin, size), size)
+            return value + grad_in[m, at, columns].astype(F32) * coef_low
+
+        def pre_copy(c):
+            return remote(
+                pre_out.at[c], pre_in.at[c], send_sem.at[7], pre_recv.at[c],
+                (r + 1 - 2 * side, f),
+            )
+
+        def pre_sum(c):
+            for m in range(count):
+                need(m, c // (chunks // 2))
+                begin = c * chunk_rows + (1 - side) * part
+                pre_out[c, m] = scaled_rows(m, begin, part, slice(0, features)).astype(BF)
+            pre_copy(c).start()
 
         def arrive(q, c, step):
             for p in range(2):
-                m, h = offset_of(q, orders[p]), c // (chunks // 2)
-                if (m, h) not in arrived:
-                    arrived.add((m, h))
-                    g_copy(m, h, w_rows(m, h).start).wait_recv()
-            for i in range(step):
-                slot = starts[i] + q
-                got(receiving.at[:, slot, chunk_at(c)], x_recv.at[slot * chunks + c])
+                need(offset_of(q, orders[p]), c // (chunks // 2))
+            if c < early and c not in arrived:
+                arrived.add(c)
+                pre_copy(c).wait_recv()
+            if step:
+                got(receiving.at[:, pl.ds(0, step), chunk_at(c)], x_recv.at[q * chunks + c])
 
         def partial(p, q, c, step):
             m = offset_of(q, orders[p])
             columns = slice(p * half, (p + 1) * half)
-            begin = pl.multiple_of(pair_begin(m) + c * chunk_rows, chunk_rows)
-            value = grad[pl.ds(begin, chunk_rows), columns] * coef
-            value = value + grad_in[m, chunk_at(c), columns].astype(F32) * coef_low
+            if c < early:
+                value = scaled_rows(m, c * chunk_rows + side * part, part, columns)
+                value = value + pre_in[c, m, :, columns].astype(F32)
+            else:
+                value = scaled_rows(m, c * chunk_rows, chunk_rows, columns)
             for i in range(step):
                 value = value + receiving[p, starts[i] + q, chunk_at(c)].astype(F32)
             return value
@@ -360,15 +399,46 @@
                 sending[p, slot, chunk_at(c)] = partial(p, keep + q, c, step).astype(BF)
                 remote(
                     sending.at[p, slot, chunk_at(c)], receiving.at[p, slot, chunk_at(c)],
-                    send_sem.at[4], x_recv.at[slot * chunks + c], across(orders[p][step]),
+                    send_sem.at[8 if c < early else 4], x_recv.at[q * chunks + c],
+                    across(orders[p][step]),
                 ).start()
+
+        def cast_copy(step, c):
+            k = 1 << step if step else 0
+            device = (lax.rem(r + k, R), f) if step else (r + 1 - 2 * side, f)
+            return remote(
+                cast_out.at[c, step], cast_in.at[c, step], send_sem.at[9],
+                cast_recv.at[c * rounds + step], device,
+            )
+
+        def cast(step, c):
+            if step == rounds - 1:
+                arrive(0, c, bits)
+                for p in range(2):
+                    own[c, 0:part, p * half:(p + 1) * half] = partial(p, 0, c, bits)
+            else:
+                cast_copy(step + 1, c).wait_recv()
+                own[c, 0:part] = own[c, 0:part] + cast_in[c, step + 1].astype(F32)
+            cast_out[c, step] = own[c, 0:part].astype(BF)
+            cast_copy(step, c).start()
+
+        def cast_total(c):
+            cast_copy(0, c).wait_recv()
+            for value, at in ((own[c, 0:part], side), (cast_in[c, 0].astype(F32), 1 - side)):
+                begin = pl.multiple_of(at * part, part)
+                if c < chunks // 2:
+                    fin_out[c, pl.ds(begin, part), :] = value
+                else:
+                    finished(value, pl.multiple_of(local(c) + begin, part))
+            if c < chunks // 2:
+                fin_copy(c).start()
 
         def z_copy(way, c, p):
             after = r + 1 - 2 * way
             columns = pl.ds(p * half, half)
             return remote(
                 chain_out.at[way, c, :, columns], chain_in.at[way, c, :, columns],
-                send_sem.at[5 + way], z_recv.at[(way * chunks + c) * 2 + p],
+                send_sem.at[5 + way], z_recv.at[(way * (chunks - early) + c - early) * 2 + p],
                 (lax.rem(after + R, R), f),
             )
 
@@ -406,7 +476,7 @@
                 fin_out[c] = value
                 fin_copy(c).start()
             else:
-                finished(value, c)
+                finished(value, local(c))
 
         def products(n):
             for m in levels[n]:
@@ -440,38 +510,51 @@
 
         period = count - 1
         final = LAG * bits
+        scattered = ending = 0
         for c in range(chunks):
+            base = period * (c - early)
+            if c < early:
+                base = period * (chunks - early + c) + ZOFF
+                at(4 * c, pre_sum, c)
             for step in range(bits):
                 keep = count >> (step + 1)
                 for q in reversed(range(keep)):
                     late = 6 if 2 * q < keep and step < bits - 1 else 0
-                    at(period * c + LAG * step + late, scatter, step, q, c)
-            at(period * c + final, gather_own, c)
+                    at(base + LAG * step + late, scatter, step, q, c)
+                    scattered = max(scattered, base + LAG * step + late)
+            if c < early:
+                for step in reversed(range(rounds)):
+                    at(base + final + CAST + (rounds - 1 - step) * NEXT, cast, step, c)
+                at(base + final + CAST + rounds * HOP, cast_total, c)
+                continue
+            at(base + final, gather_own, c)
             for hop in range(R - 1):
-                at(period * c + final + HOP * hop, relay, hop, c)
-            at(period * c + final + HOP * (R - 1), total_of, c)
-        scattered = period * (chunks - 1) + LAG * (bits - 1)
-        ending = period * (chunks - 1) + final + HOP * (R - 1)
+                at(base + final + HOP * hop, relay, hop, c)
+            at(base + final + HOP * (R - 1), total_of, c)
+            ending = max(ending, base + final + HOP * (R - 1))
         at(final, weight_first)
         at(final, products, 0)
-        at(scattered, weight_second)
-        at(scattered + 5, open_gate)
+        at(scattered + SECOND, weight_second)
+        at(scattered + 2, open_gate)
         for n in range(1, bits + 1):
-            late = (bits - n) * HOP
-            at(ending - 14 - late, weight_level, n)
-            at(ending - 7 - late, products, n)
-        at(ending - 7, key_values)
+            at(ending - 7 - 6 * (bits - n), weight_level, n)
+            at(ending - 2 - 4 * (bits - n), products, n)
+        at(ending - 2, key_values)
         for _, _, action, arguments in sorted(events, key=lambda e: e[:2]):
             action(*arguments)
         grad_gain()
         finish_weight()
         sent(fin_out, send_sem.at[2])
         sent(scal_in, send_sem.at[3])
-        sent(sending, send_sem.at[4])
+        sent(sending.at[:, :, pl.ds(0, (chunks - early) * chunk_rows)], send_sem.at[4])
+        if early:
+            sent(pre_out, send_sem.at[7])
+            sent(sending.at[:, :, pl.ds(0, early * part)], send_sem.at[8])
+            sent(cast_in, send_sem.at[9])
         for way in range(2):
             @pl.when(place(way) < R - 1)
             def _(way=way):
-                sent(chain_out.at[way], send_sem.at[5 + way])
+                sent(chain_out.at[way, pl.ds(0, chunks - early)], send_sem.at[5 + way])
 
 
 def writer(*refs):
@@ -495,13 +578,17 @@
     chunk_rows = max(pair // 8, 16)
     chunks = pair // chunk_rows
     wire = BF if R <= 4 else F32
+    early = EARLY if R in (2, 4) else 0
+    some = max(early, 1)
+    part = chunk_rows // 2
+    rounds = max(R.bit_length() - 1, 1)
     slots = sum(len(stage) for stage in stages)
     vmem = pl.BlockSpec(memory_space=pltpu.VMEM)
     hbm = pl.BlockSpec(memory_space=pltpu.HBM)
     smem = pl.BlockSpec(memory_space=pltpu.SMEM)
     dma = pltpu.SemaphoreType.DMA
     key_values, grad_weight, grad_gain = pl.pallas_call(
-        functools.partial(kernel, R, F, chunk_rows),
+        functools.partial(kernel, R, F, chunk_rows, early),
         out_shape=(
             jax.ShapeDtypeStruct((1, seq, features), BF),
             jax.ShapeDtypeStruct((rows, features), F32),
@@ -524,6 +611,10 @@
             pltpu.VMEM((chunks, chunk_rows, features), F32),
             pltpu.VMEM((2, chunks, chunk_rows, features), wire),
             pltpu.VMEM((2, chunks, chunk_rows, features), wire),
+            pltpu.VMEM((some, count, part, features), BF),
+            pltpu.VMEM((some, count, part, features), BF),
+            pltpu.VMEM((some, rounds, part, features), BF),
+            pltpu.VMEM((some, rounds, part, features), BF),
             pltpu.VMEM((chunks // 2, chunk_rows, features), F32),
             pltpu.VMEM((chunks // 2, chunk_rows, features), F32),
             pltpu.VMEM((len(stages), 1, 128), F32),
@@ -534,12 +625,14 @@
             pltpu.VMEM((rows, 1), F32),
             pltpu.VMEM((rows, 128), F32),
             dma((4,)),
-            dma((7,)),
+            dma((10,)),
             dma((2 * count,)),
             dma((count,)),
-            dma((2 * count,)),
-            dma((max(count - 1, 1) * chunks,)),
-            dma((4 * chunks,)),
+            dma((2,)),
+            dma((max(count // 2, 1) * chunks,)),
+            dma((4 * (chunks - early),)),
+            dma((some,)),
+            dma((some * rounds,)),
             dma((chunks // 2,)),
             dma((1 + len(stages),)),
             pltpu.SemaphoreType.REGULAR,

time: 31.9 us -> 31.3 us (0.981)
  Pallas kernels: 29.2 us -> 28.4 us
    pallas_call x1, Pallas kernels: 28.2 us -> 27.4 us  [shards(): pl.pallas_call(functools.partial(kernel, R, F, chunk_rows, early), out_sh...]
where the time goes in v4:
time: 31.3 us; the launch traced here: 30.9 us
  Pallas kernels  28.4 us (91%)
  between operations  2.58 us (8%)
    pallas_call x1, Pallas kernels, shards(): pl.pallas_call(functools.partial(kernel, R, F, chunk_rows, early), out_sh...  27.4 us
    pallas_call x1, Pallas kernels, shards(): pl.pallas_call(writer, out_shape=(jax.ShapeDtypeStruct(key_values.shape,...  0.91 us

profile of v4, /device:TPU:1, one launch (start us, length us, event | category | flops | bytes accessed | tf_op | source)
XLA Modules:
  0.0 30.9 jit_solution(16363083923988353294)
XLA Ops:
  2.6 27.4 %shard_map.94 = (bf16[1,256,512]{2,1,0:T(8,128)(2,1)S(1)}, f32[256,512]{1,0:T(8,128)S(1)}, f32[1,256]{1,0:T(1,128)S(1)}) custom-call(bf16[1,256,2048]{2,1,0:T(8,128)(2,1)} %states_hbm.1, bf16[1,256,512]{2,1,0:T(8,128)(2,1)} %cot_hbm.1, bf16[256,512]{1,0:T(8,128)(2,1)} %weight_hbm.1, bf16[256]{0:T(256)(128)(2,1)} %gain_hbm.1, s32[1]{0:T(128)S(6)} %copy.10.prompt_ref, ...), custom_call_target="tpu_custom_call" | custom-call | tf_op jit(solution)/shard_map/pallas_call | solution.py:590
  30.0 0.9 %shard_map.95 = (bf16[1,256,512]{2,1,0:T(8,128)(2,1)}, f32[256,512]{1,0:T(8,128)}, f32[1,256]{1,0:T(1,128)}) custom-call(bf16[1,256,512]{2,1,0:T(8,128)(2,1)S(1)} %get-tuple-element.9.refs_0_, f32[256,512]{1,0:T(8,128)S(1)} %get-tuple-element.10.refs_1_, f32[1,256]{1,0:T(1,128)S(1)} %get-tuple-element.11.refs_2_), custom_call_target="tpu_custom_call" | custom-call | tf_op jit(solution)/shard_map/pallas_call | solution.py:650

commit v5 on v4

--- a/solution.py
+++ b/solution.py
@@ -15,6 +15,7 @@
 LAG = 11
 HOP = 8
 CAST = -5
+FIRST = -3.5
 NEXT = 9
 ZOFF = 1
 SECOND = 0
@@ -515,7 +516,7 @@
             base = period * (c - early)
             if c < early:
                 base = period * (chunks - early + c) + ZOFF
-                at(4 * c, pre_sum, c)
+                at(6 * c + 4, pre_sum, c)
             for step in range(bits):
                 keep = count >> (step + 1)
                 for q in reversed(range(keep)):
@@ -524,7 +525,7 @@
                     scattered = max(scattered, base + LAG * step + late)
             if c < early:
                 for step in reversed(range(rounds)):
-                    at(base + final + CAST + (rounds - 1 - step) * NEXT, cast, step, c)
+                    at(base + final + (FIRST if step == rounds - 1 else CAST + (rounds - 1 - step) * NEXT), cast, step, c)
                 at(base + final + CAST + rounds * HOP, cast_total, c)
                 continue
             at(base + final, gather_own, c)

time: 31.3 us -> 31.1 us (level)
  no operation moved by 1% of the time
where the time goes in v5:
time: 31.1 us; the launch traced here: 30.8 us
  Pallas kernels  28.2 us (91%)
  between operations  2.58 us (8%)
    pallas_call x1, Pallas kernels, shards(): pl.pallas_call(functools.partial(kernel, R, F, chunk_rows, early), out_sh...  27.3 us
    pallas_call x1, Pallas kernels, shards(): pl.pallas_call(writer, out_shape=(jax.ShapeDtypeStruct(key_values.shape,...  0.91 us

profile of v5, /device:TPU:1, one launch (start us, length us, event | category | flops | bytes accessed | tf_op | source)
XLA Modules:
  0.0 30.8 jit_solution(5490405378745545403)
XLA Ops:
  2.6 27.3 %shard_map.94 = (bf16[1,256,512]{2,1,0:T(8,128)(2,1)S(1)}, f32[256,512]{1,0:T(8,128)S(1)}, f32[1,256]{1,0:T(1,128)S(1)}) custom-call(bf16[1,256,2048]{2,1,0:T(8,128)(2,1)} %states_hbm.1, bf16[1,256,512]{2,1,0:T(8,128)(2,1)} %cot_hbm.1, bf16[256,512]{1,0:T(8,128)(2,1)} %weight_hbm.1, bf16[256]{0:T(256)(128)(2,1)} %gain_hbm.1, s32[1]{0:T(128)S(6)} %copy.10.prompt_ref, ...), custom_call_target="tpu_custom_call" | custom-call | tf_op jit(solution)/shard_map/pallas_call | solution.py:591
  29.9 0.9 %shard_map.95 = (bf16[1,256,512]{2,1,0:T(8,128)(2,1)}, f32[256,512]{1,0:T(8,128)}, f32[1,256]{1,0:T(1,128)}) custom-call(bf16[1,256,512]{2,1,0:T(8,128)(2,1)S(1)} %get-tuple-element.9.refs_0_, f32[256,512]{1,0:T(8,128)S(1)} %get-tuple-element.10.refs_1_, f32[1,256]{1,0:T(1,128)S(1)} %get-tuple-element.11.refs_2_), custom_call_target="tpu_custom_call" | custom-call | tf_op jit(solution)/shard_map/pallas_call | solution.py:651
